TPU v7x, 32 devices: a whole 2x2x4 slice. The times are simulated.
32 devices in a mesh: seq: 8 (over z, y), fsdp: 4 (over x, core).
Axes of the slice: x: 2, y: 2, z: 4, core: 2. Of those that a mesh axis runs over, the one named last changes fastest.
Arguments:
- queries: bfloat16 [2048, 2048], P('seq', 'fsdp'), may hold values from -2.5 to 2.5
- keys_values: bfloat16 [2048, 512], P('seq', 'fsdp'), may hold values from -2.5 to 2.5
- hidden_in: bfloat16 [2048, 2880], P(('seq', 'fsdp')), may hold values from -6 to 6
- out_weight: bfloat16 [2048, 2880], P('fsdp'), may hold values from -0.5 to 0.5
- norm_gain: float32 [2880], replicated, may hold values from 0.1 to 1.9
- router_weight: bfloat16 [2880, 8], replicated, may hold values from -0.109375 to 0.109375
- expert_ids: int32 [2048, 4], P(('seq', 'fsdp')), may hold values from 0 to 7, all different within a row; in each aligned block of 64 rows (0 to 63, 64 to 127, ...) at most 64 rows name the same one
- expert_gate: bfloat16 [8, 2880, 1536], P('seq', None, 'fsdp'), may hold values from -0.109375 to 0.109375
- expert_up: bfloat16 [8, 2880, 1536], P('seq', None, 'fsdp'), may hold values from -0.109375 to 0.109375
- expert_down: bfloat16 [8, 2880, 1536], P('seq', None, 'fsdp'), may hold values from -0.15625 to 0.15625
Outputs:
- layer_out: bfloat16 [2048, 2880], P(('seq', 'fsdp'))
Inputs may be any that keep to these rules, and one draw needn't show every extreme that they name: `expert_ids`: A row names 4 different experts. Within the rows of one device (aligned blocks of 64 rows) no expert is named by more than 64 rows, a bound that some block reaches.
All inputs are finite; a program needn't handle non-finite values.
Results may differ from a plain program's by a relative error of at most 0.0075.
Values may be sent and summed in bfloat16 or wider, within the bound.
A program may use at most 128 MiB of HBM per device.

v0:
```python
import math

import jax
import jax.numpy as jnp
from jax import lax
from jax.sharding import PartitionSpec as P

D = 2880
HD = 64
WINDOW = 128
TOPK = 4


def shifted(shard, axis, by):
    count = lax.axis_size(axis)
    pairs = [(i, i + by) for i in range(count) if 0 <= i + by < count]
    return lax.ppermute(shard, axis, pairs)


def swiglu_piece(row_block, gate_part, up_part):
    gate_vals = jnp.dot(row_block, gate_part, preferred_element_type=jnp.float32)
    up_vals = jnp.dot(row_block, up_part, preferred_element_type=jnp.float32)
    return (gate_vals * jax.nn.sigmoid(1.702 * gate_vals) * (up_vals + 1.0)).astype(jnp.bfloat16)


def down_piece(hidden, down_part):
    return jnp.einsum("nk,dk->nd", hidden, down_part, preferred_element_type=jnp.float32)


def expert_rows(row_block, gate_part, up_part, down_part):
    hidden = swiglu_piece(
        row_block,
        lax.all_gather(gate_part, "fsdp", axis=1, tiled=True),
        lax.all_gather(up_part, "fsdp", axis=1, tiled=True),
    )
    combined = down_piece(hidden, lax.all_gather(down_part, "fsdp", axis=1, tiled=True))
    return combined.astype(jnp.bfloat16)


def per_device(
    queries,
    keys_values,
    hidden_in,
    out_weight,
    norm_gain,
    router_weight,
    expert_ids,
    expert_gate,
    expert_up,
    expert_down,
):
    tok_dev = queries.shape[0]
    kv_heads = keys_values.shape[1] // (2 * HD)
    heads_local = queries.shape[1] // HD
    groups = heads_local // kv_heads
    key_rim = shifted(keys_values[tok_dev - WINDOW :], "seq", 1)
    extended = jnp.concatenate([key_rim, keys_values], axis=0).reshape(
        WINDOW + tok_dev, kv_heads, 2, HD
    )
    grouped = queries.reshape(tok_dev, kv_heads, groups, HD)
    scores = jnp.einsum(
        "tkgd,skd->kgts", grouped, extended[:, :, 0], preferred_element_type=jnp.float32
    ) * (1.0 / math.sqrt(HD))
    first_pos = lax.axis_index("seq") * tok_dev
    query_pos = first_pos + jnp.arange(tok_dev, dtype=jnp.int32)
    key_pos = first_pos - WINDOW + jnp.arange(WINDOW + tok_dev, dtype=jnp.int32)
    offset = query_pos[:, None] - key_pos[None, :]
    allowed = (offset >= 0) & (offset <= WINDOW) & (key_pos[None, :] >= 0)
    raised = jnp.where(allowed, jnp.exp(scores), 0.0)
    attn_probs = (raised / jnp.sum(raised, axis=-1, keepdims=True)).astype(jnp.bfloat16)
    mixed_heads = jnp.einsum(
        "kgts,skd->tkgd", attn_probs, extended[:, :, 1], preferred_element_type=jnp.float32
    )
    attended = mixed_heads.astype(jnp.bfloat16).reshape(tok_dev, heads_local * HD)
    partial_value = jnp.dot(attended, out_weight, preferred_element_type=jnp.float32)
    rows_dev = tok_dev // lax.axis_size("fsdp")
    projected = lax.psum_scatter(partial_value, "fsdp", scatter_dimension=0, tiled=True)
    stream = (hidden_in.astype(jnp.float32) + projected).astype(jnp.bfloat16)
    stream = lax.optimization_barrier(stream)
    stream_wide = stream.astype(jnp.float32)
    inverse = lax.rsqrt(jnp.mean(stream_wide * stream_wide, axis=1, keepdims=True) + 1e-05)
    normed = (stream_wide * inverse * norm_gain).astype(jnp.bfloat16)
    experts = router_weight.shape[1]
    logits = jnp.dot(normed, router_weight, preferred_element_type=jnp.float32)
    chosen = expert_ids[:, :, None] == jnp.arange(experts, dtype=jnp.int32)[None, None, :]
    picked = jnp.sum(jnp.where(chosen, logits[:, None, :], 0.0), axis=2)
    raised_gates = jnp.exp(picked)
    gates = raised_gates / jnp.sum(raised_gates, axis=1, keepdims=True)
    flat_ids = expert_ids.reshape(-1)
    onehot = (flat_ids[:, None] == jnp.arange(experts, dtype=jnp.int32)[None, :]).astype(jnp.int32)
    running = jnp.cumsum(onehot, axis=0, dtype=jnp.int32) - onehot
    slot_ids = jnp.sum(running * onehot, axis=1, dtype=jnp.int32)
    capacity = 2 * tok_dev * TOPK // (lax.axis_size("fsdp") * experts)
    sources = jnp.repeat(normed, TOPK, axis=0)
    outgoing = jnp.zeros((experts, capacity, D), jnp.bfloat16).at[flat_ids, slot_ids].set(sources)
    owners = lax.axis_size("seq")
    per_owner = experts // owners
    outgoing = outgoing.reshape(owners, per_owner, capacity, D)
    received = lax.all_to_all(outgoing, "seq", split_axis=0, concat_axis=0, tiled=True)
    items_now = received.shape[2]
    row_block = received[:, 0].reshape(owners * items_now, D)
    answer = expert_rows(row_block, expert_gate[0], expert_up[0], expert_down[0])
    results = [answer.reshape(owners, items_now, D)]
    processed = jnp.stack(results, axis=1)
    returned = lax.all_to_all(processed, "seq", split_axis=0, concat_axis=0, tiled=True)
    return_table = returned.reshape(experts * capacity, D)
    fetched = (
        return_table[flat_ids * capacity + slot_ids].astype(jnp.float32).reshape(rows_dev, TOPK, D)
    )
    expert_sum = jnp.sum(fetched * gates[:, :, None], axis=1)
    return (stream_wide + expert_sum).astype(jnp.bfloat16)


def solution(mesh):
    return jax.shard_map(
        per_device,
        mesh=mesh,
        in_specs=(
            P("seq", "fsdp"),
            P("seq", "fsdp"),
            P(("seq", "fsdp"), None),
            P("fsdp", None),
            P(),
            P(),
            P(("seq", "fsdp"), None),
            P("seq", None, "fsdp"),
            P("seq", None, "fsdp"),
            P("seq", None, "fsdp"),
        ),
        out_specs=P(("seq", "fsdp"), None),
        check_vma=False,
    )
```

profile of v0, /device:TPU:0, one launch (start us, length us, event | category | flops | bytes accessed | tf_op | source)
XLA Modules:
  0.0 360.4 jit_solution(18101691053432819383)
XLA Ops:
  6.5 0.9 slice.15
  7.5 4.9 %collective-permute-start = (bf16[128,128]{1,0:T(8,128)(2,1)S(1)}, bf16[128,128]{1,0:T(8,128)(2,1)S(1)}, u32[]{:S(2)}, u32[]{:S(2)}) collective-permute-start(bf16[128,128]{1,0:T(8,128)(2,1)S(1)} %slice.15), channel_id=1, source_target_pairs={{0,4},{4,8},{8,12},{12,16},{16,20},{20,24},{24,28},{1,5},{5,9},{9,... | collective-permute-start | bytes 98312 | tf_op jit(solution)/shard_map/ppermute | solution.py:17
  12.6 1.1 copy.37
  13.9 0.8 pad_maximum_fusion
  14.9 0.8 fusion.18
  15.8 0.9 fusion.24
  16.6 2.6 fusion.42
  19.4 0.7 all-gather.7.cloned.1.call-update
  22.8 35.7 %reduce-scatter.2.cloned.1.call-done = f32[64,2880]{1,0:T(8,128)} async-done(((f32[256,2880]{1,0:T(8,128)}), f32[64,2880]{1,0:T(8,128)}) %reduce-scatter.2.cloned.1.call-update) | async-done | bytes 737296 | tf_op jit(solution)/shard_map/reduce_scatter | solution.py:77
  58.5 1.2 add_convert_fusion
  60.5 1.6 reshape.197
  62.5 40.6 %scatter_fusion = bf16[8,64,2880]{2,1,0:T(8,128)(2,1)S(1)} fusion(bf16[8,64,2880]{2,1,0:T(8,128)(2,1)S(1)} %broadcast_in_dim.26, s32[256]{0:T(256)S(1)} %bitcast.82, bf16[256,2880]{1,0:T(8,128)(2,1)} %reshape.197), kind=kCustom, calls=%fused_computation.1 | custom fusion | bytes 4425728 | tf_op jit(solution)/shard_map/scatter | solution.py:95
  103.2 73.5 %all_to_all.10 = bf16[8,1,64,2880]{3,2,1,0:T(8,128)(2,1)} all-to-all(bf16[8,1,64,2880]{3,2,1,0:T(8,128)(2,1)S(1)} %bitcast.80), channel_id=1, replica_groups=mesh['seq'=8,'fsdp'=4] {'seq'}, dimensions={0} | all-to-all | bytes 5898240 | tf_op jit(solution)/shard_map/all_to_all | solution.py:99
  176.6 10.6 %fusion.4 = f32[512,1536]{1,0:T(8,128)} fusion(bf16[512,2880]{1,0:T(8,128)(2,1)} %bitcast.84, bf16[1,2880,1536]{2,1,0:T(8,128)(2,1)} %all-gather.7.cloned.1.call-done), kind=kOutput, calls=%fused_computation.6 | convolution fusion | flops 4529848320 | bytes 14942208 | tf_op jit(solution)/shard_map/dot_general | solution.py:21
  187.2 58.2 %all-gather.9.cloned.1.call-done = bf16[1,2880,1536]{2,1,0:T(8,128)(2,1)} async-done(((bf16[1,2880,384]{2,1,0:T(8,128)(2,1)}), bf16[1,2880,1536]{2,1,0:T(8,128)(2,1)}) %all-gather.9.cloned.1.call-update) | async-done | bytes 8847376 | tf_op jit(solution)/shard_map/all_gather | solution.py:34
  245.4 18.4 %fusion.6 = bf16[512,2880]{0,1:T(8,128)(2,1)} fusion(bf16[1,2880,1536]{2,1,0:T(8,128)(2,1)} %all-gather.11.cloned.1.call-done, bf16[512,2880]{1,0:T(8,128)(2,1)S(1)} %bitcast.85, bf16[1,2880,1536]{2,1,0:T(8,128)(2,1)} %all-gather.9.cloned.1.call-done, f32[512,1536]{1,0:T(8,128)} %fusion.4), kind=kOutput, calls=%fused_computation.8 | convolution fusion | flops 9067462656 | bytes 26738688 | tf_op jit(solution)/shard_map/nk,dk->nd/dot_general | solution.py:27
  263.8 4.6 %copy.42 = bf16[512,2880]{1,0:T(8,128)(2,1)} copy(bf16[512,2880]{0,1:T(8,128)(2,1)} %fusion.6) | data formatting | bytes 5898240 | tf_op jit(solution)/shard_map/convert_element_type | solution.py:37
  268.4 5.6 %all-to-all-start.1 = ((bf16[8,1,64,2880]{3,2,1,0:T(8,128)(2,1)}), bf16[8,1,64,2880]{3,2,1,0:T(8,128)(2,1)S(1)}, u32[]{:S(2)}, u32[]{:S(2)}) async-start(bf16[8,1,64,2880]{3,2,1,0:T(8,128)(2,1)} %bitcast.83), calls=%async_computation.2 | async-start | bytes 6029312 | tf_op jit(solution)/shard_map/all_to_all | solution.py:105
  274.0 1.2 fusion.43
  275.4 66.9 %all-to-all-done.1 = bf16[8,1,64,2880]{3,2,1,0:T(8,128)(2,1)S(1)} async-done(((bf16[8,1,64,2880]{3,2,1,0:T(8,128)(2,1)}), bf16[8,1,64,2880]{3,2,1,0:T(8,128)(2,1)S(1)}, u32[]{:S(2)}, u32[]{:S(2)}) %all-to-all-start.1) | async-done | bytes 2949152 | tf_op jit(solution)/shard_map/all_to_all | solution.py:105
  342.3 2.7 gather_fusion
  345.0 4.1 %reshape.186 = f32[64,4,2880]{2,1,0:T(4,128)} reshape(bf16[256,2880]{1,0:T(8,128)(2,1)} %gather_fusion) | data formatting | bytes 4423680 | tf_op jit(solution)/shard_map/convert_element_type | solution.py:108
  349.1 4.0 %multiply_reduce_fusion = f32[64,2880]{1,0:T(8,128)S(1)} fusion(f32[64,4,2880]{2,1,0:T(4,128)} %reshape.186, f32[64,4]{1,0:T(8,128)S(1)} %copy.44), kind=kLoop, calls=%fused_computation.13 | loop fusion | flops 1290240 | bytes 3687424 | tf_op jit(solution)/shard_map/reduce_sum | solution.py:110
  353.0 0.8 fusion.30
  (52 shorter events, 4.6 us)
Async XLA Ops:
  6.5 10.1 %copy-start = (bf16[512,2880]{0,1:T(8,128)(2,1)S(1)}, bf16[512,2880]{0,1:T(8,128)(2,1)}, u32[]{:S(2)}) copy-start(bf16[512,2880]{0,1:T(8,128)(2,1)} %param.13) | copy-start | bytes 8847364
  6.5 52.0 %reduce-scatter.2.cloned.1.call-start = ((), (), s32[]{:S(2)}) async-start(), calls=%async_computation.3 | async-start | bytes 3768320 | tf_op jit(solution)/shard_map/reduce_scatter | solution.py:77
  7.5 6.5 %collective-permute-start = (bf16[128,128]{1,0:T(8,128)(2,1)S(1)}, bf16[128,128]{1,0:T(8,128)(2,1)S(1)}, u32[]{:S(2)}, u32[]{:S(2)}) collective-permute-start(bf16[128,128]{1,0:T(8,128)(2,1)S(1)} %slice.15), channel_id=1, source_target_pairs={{0,4},{4,8},{8,12},{12,16},{16,20},{20,24},{24,28},{1,5},{5,9},{9,... | collective-permute-start | bytes 98312 | tf_op jit(solution)/shard_map/ppermute | solution.py:17
  19.3 2.1 copy-start.7
  19.3 39.2 %copy-start.4 = (bf16[64,2880]{1,0:T(8,128)(2,1)S(1)}, bf16[64,2880]{1,0:T(8,128)(2,1)}, u32[]{:S(2)}) copy-start(bf16[64,2880]{1,0:T(8,128)(2,1)} %param.12) | copy-start | bytes 1105924
  19.3 157.3 %all-gather.7.cloned.1.call-start = ((), (), s32[]{:S(2)}) async-start(), calls=%async_computation.4 | async-start | bytes 11059200 | tf_op jit(solution)/shard_map/all_gather | solution.py:33
  20.1 39.9 %copy-start.6 = (f32[2880]{0:T(1024)S(1)}, f32[2880]{0:T(1024)}, u32[]{:S(2)}) copy-start(f32[2880]{0:T(1024)} %param.14) | copy-start | bytes 34564
  20.1 167.1 %all-gather.11.cloned.1.call-start = ((), (), s32[]{:S(2)}) async-start(), calls=%async_computation.6 | async-start | bytes 11059200 | tf_op jit(solution)/shard_map/all_gather | solution.py:36
  20.8 224.6 %all-gather.9.cloned.1.call-start = ((), (), s32[]{:S(2)}) async-start(), calls=%async_computation.5 | async-start | bytes 11059200 | tf_op jit(solution)/shard_map/all_gather | solution.py:34
  60.1 2.0 copy-start.2
  176.6 68.8 %copy-start.3 = (bf16[8,1,64,2880]{3,2,1,0:T(8,128)(2,1)S(1)}, bf16[8,1,64,2880]{3,2,1,0:T(8,128)(2,1)}, u32[]{:S(2)}) copy-start(bf16[8,1,64,2880]{3,2,1,0:T(8,128)(2,1)} %all_to_all.10) | copy-start | bytes 8847364
  268.4 5.7 %copy-start.5 = (bf16[2880,8]{0,1:T(8,128)(2,1)S(1)}, bf16[2880,8]{0,1:T(8,128)(2,1)}, u32[]{:S(2)}) copy-start(bf16[2880,8]{0,1:T(8,128)(2,1)} %param.15) | copy-start | bytes 138244
  268.4 74.0 %all-to-all-start.1 = ((bf16[8,1,64,2880]{3,2,1,0:T(8,128)(2,1)}), bf16[8,1,64,2880]{3,2,1,0:T(8,128)(2,1)S(1)}, u32[]{:S(2)}, u32[]{:S(2)}) async-start(bf16[8,1,64,2880]{3,2,1,0:T(8,128)(2,1)} %bitcast.83), calls=%async_computation.2 | async-start | bytes 6029312 | tf_op jit(solution)/shard_map/all_to_all | solution.py:105
  345.0 8.9 %copy-start.1 = (bf16[512,2880]{0,1:T(8,128)(2,1)S(1)}, bf16[512,2880]{0,1:T(8,128)(2,1)}, u32[]{:S(2)}) copy-start(bf16[512,2880]{0,1:T(8,128)(2,1)} %param.13) | copy-start | bytes 8847364
Sparse Core Ops, SparseCore 0:
  19.4 39.0 reduce-scatter.1
  60.1 60.7 all-gather.6
  122.4 60.7 all-gather.10
  184.6 60.7 all-gather.8
where the time goes:
time: 362 us; the launch traced here: 360 us
  waiting for transfers between devices  163 us (45%)
  blocking collectives  73.5 us (20%)
  local copies, waits for them, and re-layouts  57.2 us (16%)
  matrix products  34.5 us (10%)
  between operations  13.3 us (4%)
  starting transfers between devices  10.7 us (3%)
  other arithmetic  8.17 us (2%)
    all_to_all x1, blocking collectives, per_device(): lax.all_to_all(outgoing, 'seq', split_axis=0, concat_axis=0, tiled=True)  73.5 us
    all_to_all x1, waiting for transfers between devices, per_device(): lax.all_to_all(processed, 'seq', split_axis=0, concat_axis=0, tiled=True)  66.9 us
    all_gather x1, waiting for transfers between devices, expert_rows(): lax.all_gather(up_part, 'fsdp', axis=1, tiled=True)  58.2 us
    scatter x1, local copies, waits for them, and re-layouts, per_device(): jnp.zeros((experts, capacity, D), jnp.bfloat16).at[flat_ids, slot_ids]  40.6 us
    reduce_scatter x1, waiting for transfers between devices, per_device(): lax.psum_scatter(partial_value, 'fsdp', scatter_dimension=0, tiled=True)  35.7 us
    dot_general x1, matrix products, down_piece(): jnp.einsum('nk,dk->nd', hidden, down_part, preferred_element_type=jnp.flo...  18.4 us
    dot_general x1, matrix products, swiglu_piece(): jnp.dot(row_block, gate_part, preferred_element_type=jnp.float32)  10.6 us
  transfers between devices with their start and end apart: 6, of which 4 were waited for; matrix products, arithmetic and copies ran while one was open for 16% of the time, Pallas kernels for 0%

commit v1 on v0

--- a/solution.py
+++ b/solution.py
@@ -3,7 +3,9 @@
 import jax
 import jax.numpy as jnp
 from jax import lax
-from jax.sharding import PartitionSpec as P
+from jax.experimental import pallas as pl
+from jax.experimental.pallas import tpu as pltpu
+from jax.sharding import Mesh, PartitionSpec as P
 
 D = 2880
 HD = 64
@@ -111,22 +113,324 @@
     return (stream_wide + expert_sum).astype(jnp.bfloat16)
 
 
-def solution(mesh):
+def attention_partial(queries, keys_values, out_weight):
+    tok_dev = queries.shape[0]
+    kv_heads = keys_values.shape[1] // (2 * HD)
+    heads_local = queries.shape[1] // HD
+    groups = heads_local // kv_heads
+    key_rim = shifted(keys_values[tok_dev - WINDOW :], "seq", 1)
+    extended = jnp.concatenate([key_rim, keys_values], axis=0).reshape(
+        WINDOW + tok_dev, kv_heads, 2, HD
+    )
+    grouped = queries.reshape(tok_dev, kv_heads, groups, HD)
+    scores = jnp.einsum(
+        "tkgd,skd->kgts", grouped, extended[:, :, 0], preferred_element_type=jnp.float32
+    ) * (1.0 / math.sqrt(HD))
+    first_pos = lax.axis_index("seq") * tok_dev
+    query_pos = first_pos + jnp.arange(tok_dev, dtype=jnp.int32)
+    key_pos = first_pos - WINDOW + jnp.arange(WINDOW + tok_dev, dtype=jnp.int32)
+    offset = query_pos[:, None] - key_pos[None, :]
+    allowed = (offset >= 0) & (offset <= WINDOW) & (key_pos[None, :] >= 0)
+    raised = jnp.where(allowed, jnp.exp(scores), 0.0)
+    attn_probs = (raised / jnp.sum(raised, axis=-1, keepdims=True)).astype(jnp.bfloat16)
+    mixed_heads = jnp.einsum(
+        "kgts,skd->tkgd", attn_probs, extended[:, :, 1], preferred_element_type=jnp.float32
+    )
+    attended = mixed_heads.astype(jnp.bfloat16).reshape(tok_dev, heads_local * HD)
+    return jnp.dot(attended, out_weight, preferred_element_type=jnp.float32)
+
+
+def swapped(value, axis):
+    return lax.ppermute(value, axis, [(0, 1), (1, 0)])
+
+
+MESH = pl.DeviceIdType.MESH
+
+
+def places():
+    seq, far, pair = lax.axis_index("seq"), lax.axis_index("far"), lax.axis_index("pair")
+    deep = lax.axis_size("seq") // 2
+    return seq // 2, seq % 2, far, pair, deep
+
+
+def greet(partners):
+    barrier = pltpu.get_barrier_semaphore()
+    for partner in partners:
+        pl.semaphore_signal(barrier, inc=1, device_id=partner, device_id_type=MESH)
+    pl.semaphore_wait(barrier, len(partners))
+
+
+def remote(src, dst, sems, pos, partner):
+    return pltpu.make_async_remote_copy(
+        src_ref=src,
+        dst_ref=dst,
+        send_sem=sems.at[0, pos],
+        recv_sem=sems.at[1, pos],
+        device_id=partner,
+        device_id_type=MESH,
+    )
+
+
+def gather_kernel(in_ref, out_ref, held, z_sem, side_sem, relay_sem, own_sem):
+    z, y, x, c, deep = places()
+    half = in_ref.shape[0] // 2
+    y_dev, x_dev = (2 * z + 1 - y, x, c), (2 * z + y, 1 - x, c)
+    z_devs = [(2 * ((z + k) % deep) + y, x, c) for k in range(1, deep)]
+    greet([y_dev, x_dev, *z_devs])
+
+    def slot(zz, yy, xx):
+        return (zz * 2 + yy) * 2 + xx
+
+    mine = slot(z, y, x)
+    sent = []
+    for k in range(1, deep):
+        copy = remote(in_ref, held.at[mine], z_sem, k - 1, z_devs[k - 1])
+        copy.start()
+        sent.append(copy)
+    local = pltpu.make_async_copy(in_ref, held.at[mine], own_sem)
+    local.start()
+
+    def relay(k):
+        zz = (z + deep - k) % deep
+        from_y, from_x = slot(zz, 1 - y, x), slot(zz, y, 1 - x)
+        remote(held.at[from_y], held.at[from_y], side_sem, 2 * k, y_dev).wait_recv()
+        rows = held.at[from_y, pl.ds(0, half)]
+        copy = remote(rows, rows, relay_sem, 2 * k, x_dev)
+        copy.start()
+        sent.append(copy)
+        remote(held.at[from_x], held.at[from_x], side_sem, 2 * k + 1, x_dev).wait_recv()
+        rows = held.at[from_x, pl.ds(half, half)]
+        copy = remote(rows, rows, relay_sem, 2 * k + 1, y_dev)
+        copy.start()
+        sent.append(copy)
+
+    for k in range(deep):
+        here = slot((z + deep - k) % deep, y, x)
+        if k > 0:
+            remote(held.at[here], held.at[here], z_sem, k - 1, y_dev).wait_recv()
+        src = in_ref if k == 0 else held.at[here]
+        for side, partner in ((0, y_dev), (1, x_dev)):
+            copy = remote(src, held.at[here], side_sem, 2 * k + side, partner)
+            copy.start()
+            sent.append(copy)
+        if k > 0:
+            relay(k - 1)
+    relay(deep - 1)
+    local.wait()
+    for k in range(deep):
+        zz = (z + deep - k) % deep
+        opposite = slot(zz, 1 - y, 1 - x)
+        rows = held.at[opposite, pl.ds(0, half)]
+        remote(rows, rows, relay_sem, 2 * k, x_dev).wait_recv()
+        rows = held.at[opposite, pl.ds(half, half)]
+        remote(rows, rows, relay_sem, 2 * k + 1, y_dev).wait_recv()
+    final = pltpu.make_async_copy(held, out_ref, own_sem)
+    final.start()
+    for copy in sent:
+        copy.wait_send()
+    final.wait()
+
+
+def gather_rows(packet):
+    deep = lax.axis_size("seq") // 2
+    count = 4 * deep
+    return pl.pallas_call(
+        gather_kernel,
+        out_shape=jax.ShapeDtypeStruct((count, *packet.shape), packet.dtype),
+        in_specs=[pl.BlockSpec(memory_space=pltpu.VMEM)],
+        out_specs=pl.BlockSpec(memory_space=pl.ANY),
+        scratch_shapes=[
+            pltpu.VMEM((count, *packet.shape), packet.dtype),
+            pltpu.SemaphoreType.DMA((2, deep - 1)),
+            pltpu.SemaphoreType.DMA((2, 2 * deep)),
+            pltpu.SemaphoreType.DMA((2, 2 * deep)),
+            pltpu.SemaphoreType.DMA,
+        ],
+        compiler_params=pltpu.CompilerParams(collective_id=0, has_side_effects=True),
+    )(packet)
+
+
+def scatter_kernel(
+    in_ref, out_ref, first, second, staged, lined, arrived, f_sem, s_sem, d_sem, z_sem
+):
+    z, y, x, c, deep = places()
+    half = in_ref.shape[1] // 2
+    y_dev, x_dev = (2 * z + 1 - y, x, c), (2 * z + y, 1 - x, c)
+    z_devs = [(2 * ((z + k) % deep) + y, x, c) for k in range(1, deep)]
+    greet([y_dev, x_dev, *z_devs])
+    low, high = pl.ds(0, half), pl.ds(half, half)
+
+    def slot(k, yy, xx):
+        return (((z + k) % deep) * 2 + yy) * 2 + xx
+
+    def wide(value):
+        return value.astype(jnp.float32)
+
+    order = [*range(1, deep), 0]
+    sent = []
+
+    def send(*parts):
+        copy = remote(*parts)
+        copy.start()
+        sent.append(copy)
+
+    for k in order:
+        across = slot(k, 1 - y, 1 - x)
+        send(in_ref.at[across, low], first.at[k, 0], f_sem, 2 * k, x_dev)
+        send(in_ref.at[across, high], first.at[k, 1], f_sem, 2 * k + 1, y_dev)
+        to_y, to_x = slot(k, 1 - y, x), slot(k, y, 1 - x)
+        send(in_ref.at[to_y, high], second.at[k, 0, high], d_sem, 2 * k, y_dev)
+        send(in_ref.at[to_x, low], second.at[k, 1, low], d_sem, 2 * k + 1, x_dev)
+
+    def middle(k):
+        to_y, to_x = slot(k, 1 - y, x), slot(k, y, 1 - x)
+        remote(first.at[k, 0], first.at[k, 0], f_sem, 2 * k, x_dev).wait_recv()
+        staged[k, 0] = (wide(in_ref[to_y, low]) + wide(first[k, 0])).astype(staged.dtype)
+        send(staged.at[k, 0], second.at[k, 0, low], s_sem, 2 * k, y_dev)
+        remote(first.at[k, 1], first.at[k, 1], f_sem, 2 * k + 1, y_dev).wait_recv()
+        staged[k, 1] = (wide(in_ref[to_x, high]) + wide(first[k, 1])).astype(staged.dtype)
+        send(staged.at[k, 1], second.at[k, 1, high], s_sem, 2 * k + 1, x_dev)
+
+    def last(k):
+        for side, part, sem, partner in (
+            (0, low, s_sem, y_dev),
+            (0, high, d_sem, y_dev),
+            (1, high, s_sem, x_dev),
+            (1, low, d_sem, x_dev),
+        ):
+            ref = second.at[k, side, part]
+            remote(ref, ref, sem, 2 * k + side, partner).wait_recv()
+        total = wide(in_ref[slot(k, y, x)]) + wide(second[k, 0]) + wide(second[k, 1])
+        if k == 0:
+            out_ref[...] = total
+        else:
+            lined[k - 1] = total.astype(lined.dtype)
+            send(lined.at[k - 1], arrived.at[k - 1], z_sem, k - 1, z_devs[k - 1])
+
+    for pos in range(deep + 1):
+        if pos < deep:
+            middle(order[pos])
+        if pos > 0:
+            last(order[pos - 1])
+    for k in range(1, deep):
+        remote(arrived.at[k - 1], arrived.at[k - 1], z_sem, k - 1, z_devs[k - 1]).wait_recv()
+        out_ref[...] += wide(arrived[k - 1])
+    for copy in sent:
+        copy.wait_send()
+
+
+def scatter_rows(answer):
+    deep = lax.axis_size("seq") // 2
+    _, rows, width = answer.shape
+    kind = answer.dtype
+    return pl.pallas_call(
+        scatter_kernel,
+        out_shape=jax.ShapeDtypeStruct((rows, width), jnp.float32),
+        in_specs=[pl.BlockSpec(memory_space=pltpu.VMEM)],
+        out_specs=pl.BlockSpec(memory_space=pltpu.VMEM),
+        scratch_shapes=[
+            pltpu.VMEM((deep, 2, rows // 2, width), kind),
+            pltpu.VMEM((deep, 2, rows, width), kind),
+            pltpu.VMEM((deep, 2, rows // 2, width), kind),
+            pltpu.VMEM((deep - 1, rows, width), kind),
+            pltpu.VMEM((deep - 1, rows, width), kind),
+            pltpu.SemaphoreType.DMA((2, 2 * deep)),
+            pltpu.SemaphoreType.DMA((2, 2 * deep)),
+            pltpu.SemaphoreType.DMA((2, 2 * deep)),
+            pltpu.SemaphoreType.DMA((2, deep - 1)),
+        ],
+        compiler_params=pltpu.CompilerParams(collective_id=1, has_side_effects=True),
+    )(answer)
+
+
+def dense_device(
+    queries,
+    keys_values,
+    hidden_in,
+    out_weight,
+    norm_gain,
+    router_weight,
+    expert_ids,
+    expert_gate,
+    expert_up,
+    expert_down,
+):
+    gates_w = (expert_gate[0], swapped(expert_gate[0], "pair"))
+    ups_w = (expert_up[0], swapped(expert_up[0], "pair"))
+    downs_w = (expert_down[0], swapped(expert_down[0], "pair"))
+    partial_value = attention_partial(queries, keys_values, out_weight)
+    rows = hidden_in.shape[0]
+    model = hidden_in.shape[1]
+    pair, far = lax.axis_index("pair"), lax.axis_index("far")
+    split = partial_value.reshape(2, 2, rows, model)
+    mine = jnp.where(pair == 0, split[:, 0], split[:, 1])
+    other = jnp.where(pair == 0, split[:, 1], split[:, 0]).astype(jnp.bfloat16)
+    halves = mine + swapped(other, "pair").astype(jnp.float32)
+    keep = jnp.where(far == 0, halves[0], halves[1])
+    give = jnp.where(far == 0, halves[1], halves[0]).astype(jnp.bfloat16)
+    projected = keep + swapped(give, "far").astype(jnp.float32)
+    stream = (hidden_in.astype(jnp.float32) + projected).astype(jnp.bfloat16)
+    stream = lax.optimization_barrier(stream)
+    stream_wide = stream.astype(jnp.float32)
+    inverse = lax.rsqrt(jnp.mean(stream_wide * stream_wide, axis=1, keepdims=True) + 1e-05)
+    normed = (stream_wide * inverse * norm_gain).astype(jnp.bfloat16)
+    experts = router_weight.shape[1]
+    logits = jnp.dot(normed, router_weight, preferred_element_type=jnp.float32)
+    ids = jnp.arange(experts, dtype=jnp.int32)
+    chosen = jnp.any(expert_ids[:, :, None] == ids[None, None, :], axis=1)
+    raised_gates = jnp.where(chosen, jnp.exp(logits), 0.0)
+    gates = raised_gates / jnp.sum(raised_gates, axis=1, keepdims=True)
+    coarse = gates.astype(jnp.bfloat16)
+    fine = (gates - coarse.astype(jnp.float32)).astype(jnp.bfloat16)
+    fill = -(model + 2 * experts) % 128
+    blank = jnp.zeros((rows, fill), jnp.bfloat16)
+    packet = jnp.concatenate([normed, coarse, fine, blank], axis=1)
+    everyone = gather_rows(packet)
+    count = everyone.shape[0]
+    everyone = everyone.reshape(count * rows, model + 2 * experts + fill)
+    tokens = everyone[:, :model]
+    tails = everyone[:, model : model + 2 * experts].astype(jnp.float32)
+    own = lax.axis_index("seq")
+    here = jnp.arange(2 * experts, dtype=jnp.int32) % experts == own
+    weight = jnp.sum(jnp.where(here[None, :], tails, 0.0), axis=1, keepdims=True)
+    total = 0.0
+    for gate_part, up_part, down_part in zip(gates_w, ups_w, downs_w):
+        total = total + down_piece(swiglu_piece(tokens, gate_part, up_part), down_part)
+    answer = (total * weight).astype(jnp.bfloat16)
+    expert_sum = scatter_rows(answer.reshape(count, rows, model))
+    return (stream_wide + expert_sum).astype(jnp.bfloat16)
+
+
+def mapped(body, mesh, fsdp):
+    every = ("seq", *fsdp)
     return jax.shard_map(
-        per_device,
+        body,
         mesh=mesh,
         in_specs=(
-            P("seq", "fsdp"),
-            P("seq", "fsdp"),
-            P(("seq", "fsdp"), None),
-            P("fsdp", None),
+            P("seq", fsdp),
+            P("seq", fsdp),
+            P(every, None),
+            P(fsdp, None),
             P(),
             P(),
-            P(("seq", "fsdp"), None),
-            P("seq", None, "fsdp"),
-            P("seq", None, "fsdp"),
-            P("seq", None, "fsdp"),
+            P(every, None),
+            P("seq", None, fsdp),
+            P("seq", None, fsdp),
+            P("seq", None, fsdp),
         ),
-        out_specs=P(("seq", "fsdp"), None),
+        out_specs=P(every, None),
         check_vma=False,
     )
+
+
+def solution(mesh):
+    owners = mesh.shape["seq"]
+
+    def run(*args):
+        experts = args[5].shape[1]
+        if experts == owners and owners == 2 * TOPK and mesh.shape["fsdp"] == 4:
+            cut = Mesh(mesh.devices.reshape(owners, 2, 2), ("seq", "far", "pair"))
+            return mapped(dense_device, cut, ("far", "pair"))(*args)
+        return mapped(per_device, mesh, ("fsdp",))(*args)
+
+    return run

time: 362 us -> 236 us (0.65)
  waiting for transfers between devices: 163 us -> 11.6 us
  Pallas kernels: 0 us -> 139 us
  blocking collectives: 73.5 us -> 0 us
  local copies, waits for them, and re-layouts: 57.2 us -> 17.3 us
  between operations: 13.3 us -> 0.2 us
  matrix products: 34.5 us -> 47.3 us
  starting transfers between devices: 10.7 us -> 6.96 us
    pallas_call x0 -> x2, Pallas kernels: none -> 139 us  [the longest x1 74.9 us: scatter_rows(): pl.pallas_call(scatter_kernel, out_shape=jax.ShapeDtypeStruct((rows, widt...]
    all_to_all x1 -> x0, blocking collectives: 73.5 us -> none  [per_device(): lax.all_to_all(outgoing, 'seq', split_axis=0, concat_axis=0, tiled=True)]
    all_to_all x1 -> x0, waiting for transfers between devices: 66.9 us -> none  [per_device(): lax.all_to_all(processed, 'seq', split_axis=0, concat_axis=0, tiled=True)]
    all_gather x3 -> x0, waiting for transfers between devices: 58.2 us -> none  [the longest x1 58.2 us: expert_rows(): lax.all_gather(up_part, 'fsdp', axis=1, tiled=True)]
    scatter x1 -> x0, local copies, waits for them, and re-layouts: 40.6 us -> none  [per_device(): jnp.zeros((experts, capacity, D), jnp.bfloat16).at[flat_ids, slot_ids]]
    reduce_scatter x1 -> x0, waiting for transfers between devices: 35.7 us -> none  [per_device(): lax.psum_scatter(partial_value, 'fsdp', scatter_dimension=0, tiled=True)]
    ppermute x0 -> x5, waiting for transfers between devices: none -> 11.4 us  [swapped(): return lax.ppermute(value, axis, [(0, 1), (1, 0)])]
    dot_general x1 -> x2, matrix products: 18.4 us -> 27 us  [down_piece(): jnp.einsum('nk,dk->nd', hidden, down_part, preferred_element_type=jnp.flo...]
  transfers between devices with their start and end apart: 6 -> 6, of which waited for: 4 -> 3; matrix products, arithmetic and copies ran while one was open for 16% -> 15% of each run, Pallas kernels for 0% -> 28%
where the time goes in v1:
time: 236 us; the launch traced here: 232 us
  Pallas kernels  139 us (59%)
  matrix products  47.3 us (20%)
  local copies, waits for them, and re-layouts  17.3 us (7%)
  waiting for transfers between devices  11.6 us (5%)
  other arithmetic  9.65 us (4%)
  starting transfers between devices  6.96 us (3%)
    pallas_call x1, Pallas kernels, scatter_rows(): pl.pallas_call(scatter_kernel, out_shape=jax.ShapeDtypeStruct((rows, widt...  74.9 us
    pallas_call x1, Pallas kernels, gather_rows(): pl.pallas_call(gather_kernel, out_shape=jax.ShapeDtypeStruct((count, *pac...  64.5 us
    dot_general x2, matrix products, down_piece(): jnp.einsum('nk,dk->nd', hidden, down_part, preferred_element_type=jnp.flo...  27 us
    dot_general x2, matrix products, swiglu_piece(): jnp.dot(row_block, gate_part, preferred_element_type=jnp.float32)  15.7 us
    ppermute x5, waiting for transfers between devices, swapped(): return lax.ppermute(value, axis, [(0, 1), (1, 0)])  11.4 us
    convert_element_type x1, local copies, waits for them, and re-layouts, dense_device(): answer = (total * weight).astype(jnp.bfloat16)  8.51 us
    ppermute x1, starting transfers between devices, shifted(): return lax.ppermute(shard, axis, pairs)  4.89 us
  transfers between devices with their start and end apart: 6, of which 3 were waited for; matrix products, arithmetic and copies ran while one was open for 15% of the time, Pallas kernels for 28%

profile of v1, /device:TPU:0, one launch (start us, length us, event | category | flops | bytes accessed | tf_op | source)
XLA Modules:
  0.0 232.4 jit_solution(5244931701692193013)
XLA Ops:
  0.0 0.9 slice.31
  0.9 4.9 %collective-permute-start = (bf16[128,128]{1,0:T(8,128)(2,1)S(1)}, bf16[128,128]{1,0:T(8,128)(2,1)S(1)}, u32[]{:S(2)}, u32[]{:S(2)}) collective-permute-start(bf16[128,128]{1,0:T(8,128)(2,1)S(1)} %slice.31), channel_id=1, source_target_pairs={{0,4},{4,8},{8,12},{12,16},{16,20},{20,24},{24,28},{1,5},{5,9},{9,... | collective-permute-start | bytes 98312 | tf_op jit(solution)/shard_map/ppermute | solution.py:19
  6.0 1.1 copy.39
  9.2 1.6 fusion.23
  10.8 1.2 reshape.94
  12.0 1.8 fusion.8
  13.9 1.6 copy-done.1
  15.5 1.0 fusion.37
  16.5 2.6 %collective-permute-done.1 = bf16[2,64,2880]{2,1,0:T(8,128)(2,1)} collective-permute-done((bf16[2,64,2880]{2,1,0:T(8,128)(2,1)}, bf16[2,64,2880]{2,1,0:T(8,128)(2,1)}, u32[]{:S(2)}, u32[]{:S(2)}) %collective-permute-start.1) | collective-permute-done | bytes 737312 | tf_op jit(solution)/shard_map/ppermute | solution.py:144
  19.1 2.2 bitcast_add_fusion
  21.3 1.1 copy-done.2
  22.5 1.6 collective-permute-start.2
  24.7 8.8 %collective-permute-done.2 = bf16[64,2880]{1,0:T(8,128)(2,1)} collective-permute-done((bf16[64,2880]{1,0:T(8,128)(2,1)S(1)}, bf16[64,2880]{1,0:T(8,128)(2,1)}, u32[]{:S(2)}, u32[]{:S(2)}) %collective-permute-start.2) | collective-permute-done | bytes 368672 | tf_op jit(solution)/shard_map/ppermute | solution.py:144
  33.5 1.7 fusion.39
  36.8 1.8 concatenate.7.in_ref
  38.6 64.5 %shard_map.100 = bf16[16,64,2944]{2,1,0:T(8,128)(2,1)} custom-call(bf16[64,2944]{1,0:T(8,128)(2,1)} %concatenate.7.in_ref), custom_call_target="tpu_custom_call" | custom-call | tf_op jit(solution)/shard_map/pallas_call | solution.py:237
  103.1 7.9 %fusion.6 = f32[1024,384]{1,0:T(8,128)} fusion(bf16[1024,2944]{1,0:T(8,128)(2,1)} %bitcast.78, bf16[1,2880,384]{2,1,0:T(8,128)(2,1)} %param.17), kind=kOutput, calls=%fused_computation.7 | convolution fusion | flops 2264924160 | bytes 9814016 | tf_op jit(solution)/shard_map/dot_general | solution.py:23
  110.9 1.2 select_reduce_fusion
  112.1 13.0 %fusion.16 = f32[1024,2880]{0,1:T(8,128)} fusion(f32[1024,384]{1,0:T(8,128)} %fusion.6, bf16[1024,2944]{1,0:T(8,128)(2,1)} %bitcast.80, bf16[1,2880,384]{2,1,0:T(8,128)(2,1)} %param.19, bf16[1,2880,384]{2,1,0:T(8,128)(2,1)} %param.18), kind=kOutput, calls=%fused_computation.20 | convolution fusion | flops 4532994048 | bytes 23822336 | tf_op jit(solution)/shard_map/nk,dk->nd/dot_general | solution.py:29
  125.1 7.9 %fusion.2 = f32[1024,384]{1,0:T(8,128)} fusion(bf16[2880,384]{1,0:T(8,128)(2,1)} %collective-permute-done.3, bf16[1024,2944]{1,0:T(8,128)(2,1)} %bitcast.81), kind=kOutput, calls=%fused_computation.3 | convolution fusion | flops 2264924160 | bytes 9814016 | tf_op jit(solution)/shard_map/dot_general | solution.py:23
  133.0 14.0 %multiply_convert_fusion = bf16[1024,2880]{0,1:T(8,128)(2,1)} fusion(f32[1024,2880]{0,1:T(8,128)} %fusion.16, bf16[2880,384]{1,0:T(8,128)(2,1)} %collective-permute-done.5, f32[1024]{0:T(1024)S(1)} %select_reduce_fusion, f32[1024,384]{1,0:T(8,128)} %fusion.2, bf16[2880,384]{1,0:T(8,128)(2,1)} %collective-permute-done.4, bf16[1024,2944]{1,0:T(8,128)(2,1)} %bitcast.82), kind=kOutput, calls=%fused_computation | convolution fusion | flops 4541841408 | bytes 29724672 | tf_op jit(solution)/shard_map/nk,dk->nd/dot_general | solution.py:29
  147.0 8.5 %copy.47 = bf16[1024,2880]{1,0:T(8,128)(2,1)} copy(bf16[1024,2880]{0,1:T(8,128)(2,1)} %multiply_convert_fusion) | data formatting | bytes 11796480 | tf_op jit(solution)/shard_map/convert_element_type | solution.py:399
  155.5 74.9 %shard_map.101 = f32[64,2880]{1,0:T(8,128)} custom-call(bf16[16,64,2880]{2,1,0:T(8,128)(2,1)} %bitcast.77), custom_call_target="tpu_custom_call" | custom-call | tf_op jit(solution)/shard_map/pallas_call | solution.py:326
  230.4 1.9 fusion.36
  (37 shorter events, 4.5 us)
Async XLA Ops:
  0.0 12.0 %copy-start = (bf16[512,2880]{0,1:T(8,128)(2,1)S(1)}, bf16[512,2880]{0,1:T(8,128)(2,1)}, u32[]{:S(2)}) copy-start(bf16[512,2880]{0,1:T(8,128)(2,1)} %param.13) | copy-start | bytes 8847364
  0.9 6.5 %collective-permute-start = (bf16[128,128]{1,0:T(8,128)(2,1)S(1)}, bf16[128,128]{1,0:T(8,128)(2,1)S(1)}, u32[]{:S(2)}, u32[]{:S(2)}) collective-permute-start(bf16[128,128]{1,0:T(8,128)(2,1)S(1)} %slice.31), channel_id=1, source_target_pairs={{0,4},{4,8},{8,12},{12,16},{16,20},{20,24},{24,28},{1,5},{5,9},{9,... | collective-permute-start | bytes 98312 | tf_op jit(solution)/shard_map/ppermute | solution.py:19
  13.8 1.6 copy-start.1
  16.5 2.6 %collective-permute-start.1 = (bf16[2,64,2880]{2,1,0:T(8,128)(2,1)}, bf16[2,64,2880]{2,1,0:T(8,128)(2,1)}, u32[]{:S(2)}, u32[]{:S(2)}) collective-permute-start(bf16[2,64,2880]{2,1,0:T(8,128)(2,1)} %fusion.37), channel_id=1, source_target_pairs={{0,1},{1,0},{2,3},{3,2},{4,5},{5,4},{6,7},{7,6},{8,9},{9,8},{10,11... | collective-permute-start | bytes 2211848 | tf_op jit(solution)/shard_map/ppermute | solution.py:144
  16.5 8.1 %copy-start.6 = (s32[64,4]{0,1:T(4,128)S(1)}, s32[64,4]{0,1:T(4,128)}, u32[]{:S(2)}) copy-start(s32[64,4]{0,1:T(4,128)} %param.16) | copy-start | bytes 3076
  21.3 1.1 copy-start.2
  22.4 13.0 %copy-start.5 = (f32[2880]{0:T(1024)S(1)}, f32[2880]{0:T(1024)}, u32[]{:S(2)}) copy-start(f32[2880]{0:T(1024)} %param.14) | copy-start | bytes 34564
  22.4 13.9 %copy-start.4 = (bf16[2880,8]{0,1:T(8,128)(2,1)S(1)}, bf16[2880,8]{0,1:T(8,128)(2,1)}, u32[]{:S(2)}) copy-start(bf16[2880,8]{0,1:T(8,128)(2,1)} %param.15) | copy-start | bytes 138244
  22.5 11.0 %collective-permute-start.2 = (bf16[64,2880]{1,0:T(8,128)(2,1)S(1)}, bf16[64,2880]{1,0:T(8,128)(2,1)}, u32[]{:S(2)}, u32[]{:S(2)}) collective-permute-start(bf16[64,2880]{1,0:T(8,128)(2,1)S(1)} %fusion.43), channel_id=1, source_target_pairs={{0,2},{2,0},{1,3},{3,1},{4,6},{6,4},{5,7},{7,5},{8,10},{10,8},{9,1... | collective-permute-start | bytes 1105928 | tf_op jit(solution)/shard_map/ppermute | solution.py:144
  24.1 108.9 %collective-permute-start.5 = (bf16[2880,384]{1,0:T(8,128)(2,1)}, bf16[2880,384]{1,0:T(8,128)(2,1)}, u32[]{:S(2)}, u32[]{:S(2)}) collective-permute-start(bf16[2880,384]{1,0:T(8,128)(2,1)} %bitcast.19), channel_id=1, source_target_pairs={{0,1},{1,0},{2,3},{3,2},{4,5},{5,4},{6,7},{7,6},{8,9},{9,8},{10,11... | collective-permute-start | bytes 6635528 | tf_op jit(solution)/shard_map/ppermute | solution.py:144
  24.1 108.9 %collective-permute-start.4 = (bf16[2880,384]{1,0:T(8,128)(2,1)}, bf16[2880,384]{1,0:T(8,128)(2,1)}, u32[]{:S(2)}, u32[]{:S(2)}) collective-permute-start(bf16[2880,384]{1,0:T(8,128)(2,1)} %bitcast.18), channel_id=1, source_target_pairs={{0,1},{1,0},{2,3},{3,2},{4,5},{5,4},{6,7},{7,6},{8,9},{9,8},{10,11... | collective-permute-start | bytes 6635528 | tf_op jit(solution)/shard_map/ppermute | solution.py:144
  24.6 100.5 %collective-permute-start.3 = (bf16[2880,384]{1,0:T(8,128)(2,1)}, bf16[2880,384]{1,0:T(8,128)(2,1)}, u32[]{:S(2)}, u32[]{:S(2)}) collective-permute-start(bf16[2880,384]{1,0:T(8,128)(2,1)} %bitcast.17), channel_id=1, source_target_pairs={{0,1},{1,0},{2,3},{3,2},{4,5},{5,4},{6,7},{7,6},{8,9},{9,8},{10,11... | collective-permute-start | bytes 6635528 | tf_op jit(solution)/shard_map/ppermute | solution.py:144
  35.6 0.7 copy-start.3
